TPU v7x, 8 devices: a whole 2x2x1 slice. The times are simulated.
8 devices in a mesh: dp: 1 (over z), ep: 8 (over x, y, core).
Axes of the slice: x: 2, y: 2, z: 1, core: 2. Of those that a mesh axis runs over, the one named last changes fastest.
Arguments:
- x: bfloat16 [1, 8, 256, 4096], P('dp', 'ep')
- expert: int32 [1, 8, 256, 8], P('dp', 'ep')
- slot: int32 [1, 8, 256, 8], P('dp', 'ep')
- gate: float32 [1, 8, 256, 8], P('dp', 'ep')
- w_gate: bfloat16 [64, 4096, 1536], P('ep')
- w_up: bfloat16 [64, 4096, 1536], P('ep')
- w_down: bfloat16 [64, 1536, 4096], P('ep')
Outputs:
- y: bfloat16 [1, 8, 256, 4096], P('dp', 'ep')
All inputs are finite; a program needn't handle non-finite values.
Results may differ from a plain program's by a relative error of at most 0.009.
Values are sent between devices in bfloat16 or wider.
A program may use at most 2 GiB of HBM per device.

v0:
```python
import functools

import jax
import jax.numpy as jnp
from jax import lax
from jax.experimental import pallas as pl
from jax.experimental.pallas import tpu as pltpu
from jax.sharding import PartitionSpec as P

MESH = pl.DeviceIdType.MESH
F32, BF16 = jnp.float32, jnp.bfloat16
CH = 512
NW = 6
H, T, M, SL, PAD, KP = 128, 256, 320, 40, 48, 384
PAIR, PT, LOW, TAB, ROWS, OUT = 80, 640, 1280, 24, 2560, 3072

AX, BX, FX, AY, BY, FY, PO, PAX, PBX, PFX, PAY, PBY, PFY = range(13)
NX, NY, NC, ME, DG = 4, 2, 1, 0, 6
KINDS = (
    (NX, ME, ME, H), (NX, ME, H, H), (NX, NY, H, H),
    (NY, ME, H, H), (NY, ME, ME, H), (NY, NX, ME, H),
    (NC, ME, ME, T), (NC, NX, ME, H), (NC, NX, H, H), (NC, DG, H, H),
    (NC, NY, H, H), (NC, NY, ME, H), (NC, DG, ME, H),
)
TABLES = ((NX, ME), (NY, ME), (DG, ME), (NC, ME), (NC, NX), (NC, NY), (NC, DG))


def dot(a, b):
    return jnp.dot(a, b, preferred_element_type=F32)


def kernel(x, table, wg, wu, wd, y, xs, acc_g, acc_u, zo, pick, mix, w, tables,
           ag_s, ag_r, tb_s, tb_r, own_sem, wsem, a_s, a_r, sx_s, sy_s, t1_r, t2_r,
           cx_s, cy_s, rx_r, ry_r, ysem, ready, cred_p, cred_x, cred_y):
    chunks = x.shape[1] // CH
    me = lax.axis_index("ep")
    mx, my, mc = me // 4, (me // 2) % 2, me % 2

    def at(mask):
        px = 1 - mx if mask & 4 else mx
        py = 1 - my if mask & 2 else my
        pc = 1 - mc if mask & 1 else mc
        return 4 * px + 2 * py + pc

    def cols(c):
        return pl.ds(pl.multiple_of(c * CH, CH), CH)

    def rows(dev, first, n):
        return pl.ds(pl.multiple_of(dev * T + first, H), n)

    def to(mask):
        return {"ep": at(mask)}

    def ag_send(kind, c):
        link, owner, first, n = KINDS[kind]
        place = xs.at[c, rows(at(owner), first, n), :]
        src = x.at[pl.ds(first, n), cols(c)] if owner == 0 else place
        return pltpu.make_async_remote_copy(
            src_ref=src, dst_ref=place, send_sem=ag_s.at[kind, c], recv_sem=ag_r.at[kind, c],
            device_id=to(link), device_id_type=MESH)

    def ag_arrive(kind, c):
        link, owner, first, n = KINDS[kind]
        place = xs.at[c, rows(at(link ^ owner), first, n), :]
        pltpu.make_async_remote_copy(
            src_ref=place, dst_ref=place, send_sem=ag_s.at[kind, c], recv_sem=ag_r.at[kind, c],
            device_id=to(link), device_id_type=MESH).wait_recv()

    def start(c, *kinds):
        for kind in kinds:
            ag_send(kind, c).start()

    def arrive(c, *kinds):
        for kind in kinds:
            ag_arrive(kind, c)

    def tb_copy(i):
        link, owner = TABLES[i]
        src = table if owner == 0 else tables.at[at(owner)]
        return pltpu.make_async_remote_copy(
            src_ref=src, dst_ref=tables.at[at(owner)], send_sem=tb_s.at[i], recv_sem=tb_r.at[i],
            device_id=to(link), device_id_type=MESH)

    def tb_arrive(i):
        link, owner = TABLES[i]
        place = tables.at[at(link ^ owner)]
        pltpu.make_async_remote_copy(
            src_ref=place, dst_ref=place, send_sem=tb_s.at[i], recv_sem=tb_r.at[i],
            device_id=to(link), device_id_type=MESH).wait_recv()

    def w_first(g):
        c, e = g // 8, g % 8
        k = pl.ds(pl.multiple_of(c * CH, CH), CH)
        s = 2 * (g % 3)
        return (pltpu.make_async_copy(wg.at[e, k, :], w.at[s], wsem.at[s]),
                pltpu.make_async_copy(wu.at[e, k, :], w.at[s + 1], wsem.at[s + 1]))

    def w_second(q):
        d, e = q // 8, q % 8
        s = (q + 2) % NW
        for k in range(3):
            pltpu.make_async_copy(
                wd.at[e, pl.ds(k * CH, CH), cols(d)], w.at[s, :, pl.ds(k * CH, CH)], wsem.at[s]
            ).start()

    def w_second_wait(q):
        s = (q + 2) % NW
        pltpu.make_async_copy(wg.at[0, pl.ds(0, CH), :], w.at[s], wsem.at[s]).wait()

    barrier = pltpu.get_barrier_semaphore()
    for mask in (4, 2, 6, 1):
        pl.semaphore_signal(barrier, inc=1, device_id=to(mask), device_id_type=MESH)
    for g in range(3):
        for copy in w_first(g):
            copy.start()
    pl.semaphore_wait(barrier, 4)

    for i in range(4):
        tb_copy(i).start()
    start(0, AX, AY, BX, BY, PO)
    for c in range(chunks):
        pltpu.make_async_copy(x.at[:, cols(c)], xs.at[c, rows(me, 0, T), :], own_sem.at[c]).start()
    tables[me] = table[...]
    @pl.loop(0, 32)
    def _(i):
        r = pl.ds(pl.multiple_of(i * PAIR, PAIR), PAIR)
        acc_g[r, :] = jnp.zeros((PAIR, acc_g.shape[1]), F32)
        acc_u[r, :] = jnp.zeros((PAIR, acc_u.shape[1]), F32)

    for i in range(3):
        tb_arrive(i)
        tb_copy(i + 4).start()
    arrive(0, AX, AY)
    start(0, FX, FY, PAX, PAY)
    start(1, AX, AY, BX, BY, PO)
    start(2, AX, AY)
    for i in range(3, 7):
        tb_arrive(i)
    for i in range(7):
        tb_copy(i).wait_send()

    eye = jnp.where(
        lax.broadcasted_iota(jnp.int32, (T, T), 0) == lax.broadcasted_iota(jnp.int32, (T, T), 1),
        1.0, 0.0).astype(BF16)
    row40 = lax.broadcasted_iota(jnp.int32, (SL, T), 0).astype(F32)
    row48 = lax.broadcasted_iota(jnp.int32, (PAD, T), 0).astype(F32)

    @pl.loop(0, 8)
    def _(s):
        mine = (lax.broadcasted_iota(jnp.int32, (8, T), 0) + me * 8).astype(F32)
        slot = jnp.full((8, T), -1000.0, F32)
        gate = jnp.zeros((8, T), F32)
        for j in range(8):
            hit = tables[s, j:j + 1, :] == mine
            slot = jnp.where(hit, tables[s, 8 + j:9 + j, :], slot)
            gate = jnp.where(hit, tables[s, 16 + j:17 + j, :], gate)
        for e in range(0, 8, 2):
            pick[s, e * SL:e * SL + PAIR, :] = jnp.concatenate(
                [jnp.where(row40 == slot[i:i + 1, :], 1.0, 0.0) for i in (e, e + 1)], 0).astype(BF16)
        for e in range(8):
            zo[e * PAD:e * PAD + PAD, 0:T] = jnp.where(
                row48 == slot[e:e + 1, :], gate[e:e + 1, :], 0.0).astype(BF16)
        mix[s] = lax.dot_general(
            eye, zo[0:KP, 0:T], (((1,), (1,)), ((), ())), preferred_element_type=F32).astype(BF16)

    arrive(0, BX, BY)
    start(0, PBX, PBY)
    arrive(0, FX, FY)
    start(0, PFX, PFY)

    def gather(c):
        pltpu.make_async_copy(x.at[:, cols(c)], xs.at[c, rows(me, 0, T), :], own_sem.at[c]).wait()
        arrive(c, PO, PAX, PAY, PBX, PBY, PFX, PFY)

        for p in range(4):
            a = dot(pick[2 * p], xs[c, p * CH:p * CH + T, :])
            b = dot(pick[2 * p + 1], xs[c, p * CH + T:p * CH + CH, :])
            for e in range(8):
                zo[e * M + p * PAIR:e * M + p * PAIR + PAIR, :] = jnp.concatenate(
                    [a[e * SL:e * SL + SL], b[e * SL:e * SL + SL]], 0).astype(BF16)

    def of_expert(e):
        return pl.ds(e * M, M)

    @pl.loop(0, chunks - 1)
    def _(c):
        gather(c)
        for e in range(8):
            g = c * 8 + e
            for copy in w_first(g):
                copy.wait()
            s = 2 * (g % 3)
            r = of_expert(e)
            z = zo[r, :]
            for k in range(0, acc_g.shape[1], CH):
                kk = pl.ds(k, CH)
                acc_g[r, kk] += dot(z, w[s, :, kk])
                acc_u[r, kk] += dot(z, w[s + 1, :, kk])
            for copy in w_first(g + 3):
                copy.start()
            if e == 0:
                arrive(c + 1, AX, AY)
                start(c + 1, FX, FY, PAX, PAY)
            if e == 2:
                @pl.when(c + 2 < chunks)
                def _():
                    start(c + 2, BX, BY, PO)
            if e == 3:
                @pl.when(c + 3 < chunks)
                def _():
                    start(c + 3, AX, AY)
            if e == 4:
                arrive(c + 1, BX, BY)
                start(c + 1, PBX, PBY)
            if e == 6:
                arrive(c + 1, FX, FY)
                start(c + 1, PFX, PFY)

    gather(chunks - 1)

    @pl.loop(0, chunks)
    def _(c):
        for kind in range(13):
            ag_send(kind, c).wait_send()

    for mask in (4, 2, 1):
        pl.semaphore_signal(ready, inc=1, device_id=to(mask), device_id_type=MESH)

    def hidden(e, k):
        return xs.at[(e // 4) * 3 + k, pl.ds((e % 4) * M, M), :]

    for e in range(8):
        g = (chunks - 1) * 8 + e
        for copy in w_first(g):
            copy.wait()
        s = 2 * (g % 3)
        r = of_expert(e)
        z = zo[r, :]
        for k in range(3):
            kk = pl.ds(k * CH, CH)
            gg = acc_g[r, kk] + dot(z, w[s, :, kk])
            uu = acc_u[r, kk] + dot(z, w[s + 1, :, kk])
            hidden(e, k)[...] = (jax.nn.silu(gg) * uu).astype(BF16)
        if e < 5:
            for copy in w_first(g + 3):
                copy.start()
        else:
            w_second(2 * (e - 5))
            w_second(2 * (e - 5) + 1)

    pl.semaphore_wait(ready, 3)

    chip = 2 * mx + my
    chip_x, chip_y, chip_d = 2 * (1 - mx) + my, 2 * mx + 1 - my, 3 - chip

    def part(d, i, first, n):
        k = d % 4
        return acc_g.at[pl.ds(pl.multiple_of((k % 2) * 1024 + i * T + first, H), n),
                        pl.ds(pl.multiple_of((k // 2) * CH, CH), CH)]

    def got_a(d, i):
        return xs.at[6, pl.ds(pl.multiple_of((d % 2) * 1024 + i * T, T), T), :]

    def put_a(d, i):
        return xs.at[7, pl.ds(pl.multiple_of((d % 2) * 1024 + i * T, T), T), :]

    def got(d, first, n):
        return xs.at[d % 4, pl.ds(LOW + first, n), :]

    def put(d, first, n):
        return xs.at[4 + d % 2, pl.ds(LOW + first, n), :]

    def send_a(d, i):
        return pltpu.make_async_remote_copy(
            src_ref=put_a(d, i), dst_ref=got_a(d, i), send_sem=a_s.at[d % 2, i], recv_sem=a_r.at[d % 2, i],
            device_id=to(1), device_id_type=MESH)

    def send_x1(d):
        return pltpu.make_async_remote_copy(
            src_ref=put(d, 0, T), dst_ref=got(d, 0, T), send_sem=sx_s.at[d % 2], recv_sem=t1_r.at[d % 4],
            device_id=to(4), device_id_type=MESH)

    def send_y1(d):
        return pltpu.make_async_remote_copy(
            src_ref=put(d, T, T), dst_ref=got(d, T, T), send_sem=sy_s.at[d % 2], recv_sem=t2_r.at[d % 4],
            device_id=to(2), device_id_type=MESH)

    def send_y2(d):
        return pltpu.make_async_remote_copy(
            src_ref=put(d, CH, H), dst_ref=got(d, CH, H), send_sem=cy_s.at[d % 2], recv_sem=ry_r.at[d % 4],
            device_id=to(2), device_id_type=MESH)

    def send_x2(d):
        return pltpu.make_async_remote_copy(
            src_ref=put(d, PT, H), dst_ref=got(d, PT, H), send_sem=cx_s.at[d % 2], recv_sem=rx_r.at[d % 4],
            device_id=to(4), device_id_type=MESH)

    def send_out(d, n):
        return pltpu.make_async_copy(
            pick.at[2 * (d % 4) + n, pl.ds(0, T), :],
            y.at[:, pl.ds(pl.multiple_of(d * CH + n * T, T), T)], ysem.at[d % 4, n])

    def step_b(d):
        for i in range(4):
            send_a(d, i).wait_recv()

        @pl.when(d >= 2)
        def _():
            send_x1(d - 2).wait_send()
            send_y1(d - 2).wait_send()

        @pl.when(d >= 4)
        def _():
            pl.semaphore_wait(cred_x, 1)
            pl.semaphore_wait(cred_y, 1)

        def total(i, first):
            return part(d, i, first, H)[...] + got_a(d, i)[pl.ds(first, H), :].astype(F32)

        put(d, 0, H)[...] = total(chip_x, 0).astype(BF16)
        put(d, H, H)[...] = total(chip_d, 0).astype(BF16)
        send_x1(d).start()
        put(d, T, H)[...] = total(chip_y, H).astype(BF16)
        put(d, KP, H)[...] = total(chip_d, H).astype(BF16)
        send_y1(d).start()
        for i, first in ((chip, 0), (chip, H), (chip_y, 0), (chip_x, H)):
            part(d, i, first, H)[...] = total(i, first)

        @pl.when(d < chunks - 2)
        def _():
            pl.semaphore_signal(cred_p, inc=1, device_id=to(1), device_id_type=MESH)

    def step_c(d):
        @pl.when(d >= 2)
        def _():
            send_x2(d - 2).wait_send()
            send_y2(d - 2).wait_send()

        send_x1(d).wait_recv()
        put(d, CH, H)[...] = (part(d, chip_y, 0, H)[...] + got(d, H, H)[...].astype(F32)).astype(BF16)
        send_y2(d).start()
        send_y1(d).wait_recv()
        put(d, PT, H)[...] = (part(d, chip_x, H, H)[...] + got(d, KP, H)[...].astype(F32)).astype(BF16)
        send_x2(d).start()

    def step_d(d):
        @pl.when(d >= 4)
        def _():
            send_out(d - 4, 0).wait()
            send_out(d - 4, 1).wait()

        send_y2(d).wait_recv()
        top = part(d, chip, 0, H)[...] + got(d, 0, H)[...].astype(F32) + got(d, CH, H)[...].astype(F32)
        send_x2(d).wait_recv()
        low = part(d, chip, H, H)[...] + got(d, T, H)[...].astype(F32) + got(d, PT, H)[...].astype(F32)
        for n in range(2):
            pick[2 * (d % 4) + n, 0:H, :] = top[:, n * T:n * T + T].astype(BF16)
            pick[2 * (d % 4) + n, H:T, :] = low[:, n * T:n * T + T].astype(BF16)
            send_out(d, n).start()

        @pl.when(d < chunks - 4)
        def _():
            pl.semaphore_signal(cred_x, inc=1, device_id=to(4), device_id_type=MESH)
            pl.semaphore_signal(cred_y, inc=1, device_id=to(2), device_id_type=MESH)

    @pl.loop(0, chunks)
    def _(d):
        for e in range(0, 8, 2):
            q = d * 8 + e
            w_second_wait(q)
            w_second_wait(q + 1)
            for i in (e, e + 1):
                s = (d * 8 + i + 2) % NW
                out = dot(hidden(i, 0)[...], w[s, :, pl.ds(0, CH)])
                out += dot(hidden(i, 1)[...], w[s, :, pl.ds(CH, CH)])
                out += dot(hidden(i, 2)[...], w[s, :, pl.ds(1024, CH)])
                for p in range(8):
                    rows48 = out[p * SL:p * SL + PAD] if p < 7 else jnp.concatenate(
                        [out[p * SL:], jnp.zeros((8, CH), F32)], 0)
                    zo[p * KP + i * PAD:p * KP + i * PAD + PAD, :] = rows48.astype(BF16)
            if e == 0:
                w_second(q + NW)
                w_second(q + NW + 1)
            else:
                @pl.when(d < chunks - 1)
                def _():
                    w_second(q + NW)
                    w_second(q + NW + 1)
            if e == 2:
                @pl.when(d >= 1)
                def _():
                    step_b(d - 1)

        @pl.when(d >= 2)
        def _():
            pl.semaphore_wait(cred_p, 1)
            for i in range(4):
                send_a(d - 2, i).wait_send()

        for i in range(4):
            o = zo[pl.ds(pl.multiple_of((2 * i + 1 - mc) * KP, KP), KP), :]
            put_a(d, i)[...] = dot(mix[2 * i + 1 - mc], o).astype(BF16)
            send_a(d, i).start()
        for i in range(4):
            o = zo[pl.ds(pl.multiple_of((2 * i + mc) * KP, KP), KP), :]
            part(d, i, 0, T)[...] = dot(mix[2 * i + mc], o)

        @pl.when(d >= 2)
        def _():
            step_c(d - 2)

        @pl.when(d >= 3)
        def _():
            step_d(d - 3)

    last = chunks - 1
    step_b(last)
    step_c(last - 1)
    step_d(last - 2)
    step_c(last)
    step_d(last - 1)
    step_d(last)
    for d in (last - 1, last):
        for i in range(4):
            send_a(d, i).wait_send()
        for copy in (send_x1(d), send_y1(d), send_x2(d), send_y2(d)):
            copy.wait_send()
    for d in range(chunks - 4, chunks):
        for n in range(2):
            send_out(d, n).wait()


def solution(mesh):
    def body(x, expert, slot, gate, w_gate, w_up, w_down):
        tokens, dim = x.shape[2:]
        ff = w_gate.shape[2]
        slots = SL
        keep = slot[0, 0] < slots
        table = jnp.concatenate([
            expert[0, 0].astype(F32).T,
            jnp.where(keep, slot[0, 0], -1000).astype(F32).T,
            gate[0, 0].astype(BF16).astype(F32).T,
        ])
        dma = pltpu.SemaphoreType.DMA
        any_ = pl.BlockSpec(memory_space=pl.ANY)
        y = pl.pallas_call(
            kernel,
            out_shape=jax.ShapeDtypeStruct((tokens, dim), BF16),
            in_specs=[any_, pl.BlockSpec(memory_space=pltpu.VMEM), any_, any_, any_],
            out_specs=any_,
            scratch_shapes=[
                pltpu.VMEM((dim // CH, 8 * tokens, CH), BF16),
                pltpu.VMEM((ROWS, ff), F32),
                pltpu.VMEM((ROWS, ff), F32),
                pltpu.VMEM((OUT, CH), BF16),
                pltpu.VMEM((8, M, T), BF16),
                pltpu.VMEM((8, T, KP), BF16),
                pltpu.VMEM((NW, CH, ff), BF16),
                pltpu.VMEM((8, TAB, T), F32),
                dma((13, dim // CH)), dma((13, dim // CH)), dma((7,)), dma((7,)),
                dma((dim // CH,)), dma((NW,)),
                dma((2, 4)), dma((2, 4)), dma((2,)), dma((2,)), dma((4,)), dma((4,)),
                dma((2,)), dma((2,)), dma((4,)), dma((4,)), dma((4, 2)),
                pltpu.SemaphoreType.REGULAR, pltpu.SemaphoreType.REGULAR,
                pltpu.SemaphoreType.REGULAR, pltpu.SemaphoreType.REGULAR,
            ],
            compiler_params=pltpu.CompilerParams(
                collective_id=0, has_side_effects=True, vmem_limit_bytes=67043328),
        )(x[0, 0], table, w_gate, w_up, w_down)
        return y[None, None]

    tok = P("dp", "ep", None, None)
    wt = P("ep", None, None)
    return jax.shard_map(
        body, mesh=mesh, in_specs=(tok, tok, tok, tok, wt, wt, wt), out_specs=tok, check_vma=False
    )
```

profile of v0, /device:TPU:0, one launch (start us, length us, event | category | flops | bytes accessed | tf_op | source)
XLA Modules:
  0.0 193.3 jit_solution(7692599725877908660)
XLA Ops:
  0.0 0.7 convert_bitcast_fusion.1
  0.7 0.7 fusion.1
  1.4 0.7 convert_bitcast_fusion
  2.1 0.6 pad_maximum_fusion.table
  2.7 187.5 %shard_map.73 = bf16[256,4096]{1,0:T(8,128)(2,1)} custom-call(bf16[256,4096]{1,0:T(8,128)(2,1)} %bitcast.16, f32[24,256]{1,0:T(8,128)} %pad_maximum_fusion.table, bf16[8,4096,1536]{2,1,0:T(8,128)(2,1)} %wg.1, bf16[8,4096,1536]{2,1,0:T(8,128)(2,1)} %wu.1, bf16[8,1536,4096]{2,1,0:T(8,128)(2,1)} %wd.1), custom_call_target="tpu_custom_call" | custom-call | tf_op jit(solution)/shard_map/pallas_call | solution.py:446
  190.2 3.1 %copy.9 = bf16[1,1,256,4096]{3,2,1,0:T(8,128)(2,1)} copy(bf16[1,1,256,4096]{3,2,1,0:T(8,128)(2,1)} %bitcast.15) | data formatting | bytes 4194304
where the time goes:
time: 194 us; the launch traced here: 193 us
  Pallas kernels  187 us (96%)
  local copies, waits for them, and re-layouts  3.13 us (2%)
  other arithmetic  2.71 us (1%)
    pallas_call x1, Pallas kernels, body(): pl.pallas_call(kernel, out_shape=jax.ShapeDtypeStruct((tokens, dim), BF16...  187 us

commit v1 on v0

v1 whole, which is shorter than its diff:
```python
import functools

import jax
import jax.numpy as jnp
from jax import lax
from jax.experimental import pallas as pl
from jax.experimental.pallas import tpu as pltpu
from jax.sharding import PartitionSpec as P

MESH = pl.DeviceIdType.MESH
F32, BF16 = jnp.float32, jnp.bfloat16
CH = 512
NW = 6
H, T, M, SL, PAD, KP = 128, 256, 320, 40, 48, 384
PAIR, PT, LOW, TAB, ROWS, OUT = 80, 640, 1280, 24, 2560, 3072

AX, BX, FX, AY, BY, FY, PO, PAX, PBX, PFX, PAY, PBY, PFY = range(13)
NX, NY, NC, ME, DG = 4, 2, 1, 0, 6
KINDS = (
    (NX, ME, ME, H), (NX, ME, H, H), (NX, NY, H, H),
    (NY, ME, H, H), (NY, ME, ME, H), (NY, NX, ME, H),
    (NC, ME, ME, T), (NC, NX, ME, H), (NC, NX, H, H), (NC, DG, H, H),
    (NC, NY, H, H), (NC, NY, ME, H), (NC, DG, ME, H),
)
TABLES = ((NX, ME), (NY, ME), (DG, ME), (NC, ME), (NC, NX), (NC, NY), (NC, DG))


def dot(a, b):
    return jnp.dot(a, b, preferred_element_type=F32)


def kernel(x, expert, slot, gate, wg, wu, wd, y, xs, acc_g, acc_u, zo, pick, w, w2, tables,
           ag_s, ag_r, tb_s, tb_r, own_sem, mix_sem, wsem, a_s, a_r, sx_s, sy_s, t1_r, t2_r,
           cx_s, cy_s, rx_r, ry_r, ysem, ready, cred_p, cred_x, cred_y):
    last = x.shape[1] // CH
    me = lax.axis_index("ep")
    mx, my, mc = me // 4, (me // 2) % 2, me % 2

    def at(mask):
        px = 1 - mx if mask & 4 else mx
        py = 1 - my if mask & 2 else my
        pc = 1 - mc if mask & 1 else mc
        return 4 * px + 2 * py + pc

    def static(c):
        return isinstance(c, int)

    def wide(c):
        return T if static(c) and c in (0, last) else CH

    def cols(c):
        if static(c):
            return pl.ds(max(c * CH - T, 0), wide(c))
        return pl.ds(pl.multiple_of(c * CH - T, T), CH)

    def when(cond, fn):
        if isinstance(cond, bool):
            if cond:
                fn()
        else:
            pl.when(cond)(fn)

    def sized(c, fn, low=True):
        if static(c):
            if 0 <= c <= last:
                fn(c)
            return
        if low:
            when(c == 0, lambda: fn(0))
            when(c > 0, lambda: fn(c))
        else:
            when(c < last, lambda: fn(c))
            when(c == last, lambda: fn(last))

    def block(c, r):
        if static(c) and c == last:
            return xs.at[0, r, T:CH]
        return xs.at[c, r, 0:wide(c)]

    def rows(dev, first, n):
        return pl.ds(pl.multiple_of(dev * T + first, H), n)

    def to(mask):
        return {"ep": at(mask)}

    def ag_send(kind, c):
        link, owner, first, n = KINDS[kind]
        place = block(c, rows(at(owner), first, n))
        src = x.at[pl.ds(first, n), cols(c)] if owner == 0 else place
        return pltpu.make_async_remote_copy(
            src_ref=src, dst_ref=place, send_sem=ag_s.at[kind, c], recv_sem=ag_r.at[kind, c],
            device_id=to(link), device_id_type=MESH)

    def ag_arrive(kind, c):
        link, owner, first, n = KINDS[kind]
        place = block(c, rows(at(link ^ owner), first, n))
        pltpu.make_async_remote_copy(
            src_ref=place, dst_ref=place, send_sem=ag_s.at[kind, c], recv_sem=ag_r.at[kind, c],
            device_id=to(link), device_id_type=MESH).wait_recv()

    def start(c, *kinds):
        for kind in kinds:
            ag_send(kind, c).start()

    def arrive(c, *kinds):
        for kind in kinds:
            ag_arrive(kind, c)

    def tb_copy(i):
        link, owner = TABLES[i]
        src = tables.at[at(owner)]
        return pltpu.make_async_remote_copy(
            src_ref=src, dst_ref=tables.at[at(owner)], send_sem=tb_s.at[i], recv_sem=tb_r.at[i],
            device_id=to(link), device_id_type=MESH)

    def tb_arrive(i):
        link, owner = TABLES[i]
        place = tables.at[at(link ^ owner)]
        pltpu.make_async_remote_copy(
            src_ref=place, dst_ref=place, send_sem=tb_s.at[i], recv_sem=tb_r.at[i],
            device_id=to(link), device_id_type=MESH).wait_recv()

    def slot_of(s):
        return w.at[s] if s < NW else w2.at[s - NW]

    def w_first(c, e):
        s = 2 * (e % 4)
        k = pl.ds(0, wide(c))
        return [pltpu.make_async_copy(m.at[e, cols(c), :], slot_of(s + i).at[k, :], wsem.at[s + i])
                for i, m in enumerate((wg, wu))]

    def w_load(c, e):
        for copy in w_first(c, e):
            copy.start()

    def w_fetch(c, pair):
        w_load(c, 2 * pair)
        w_load(c, 2 * pair + 1)

    def w_next(c, e):
        if e < 4:
            w_load(c, e + 4)
        else:
            sized(c + 1, lambda n: w_load(n, e - 4), low=False)

    def w_wait(c, pair):
        for e in (2 * pair, 2 * pair + 1):
            for copy in w_first(c, e):
                copy.wait()

    def w_second(d, e):
        s = (d * 8 + e) % NW
        for k in range(0, wg.shape[2], CH):
            pltpu.make_async_copy(
                wd.at[e, pl.ds(k, CH), cols(d)], w.at[s, :, pl.ds(k, wide(d))], wsem.at[s]).start()

    def w_second_wait(d, e):
        s = (d * 8 + e) % NW
        part = pl.ds(0, wide(d))
        pltpu.make_async_copy(wg.at[0, part, :], w.at[s, part, :], wsem.at[s]).wait()
        return s

    tables[me, 0:8, :] = expert[...].astype(F32)
    tables[me, 8:16, :] = jnp.where(slot[...] < SL, slot[...], -1000).astype(F32)
    tables[me, 16:TAB, :] = gate[...].astype(BF16).astype(F32)
    barrier = pltpu.get_barrier_semaphore()
    for mask in (4, 2, 6, 1):
        pl.semaphore_signal(barrier, inc=1, device_id=to(mask), device_id_type=MESH)
    w_fetch(0, 0)
    w_fetch(0, 1)
    pl.semaphore_wait(barrier, 4)

    for i in range(4):
        tb_copy(i).start()
    start(0, AX, AY, BX, BY, PO)
    def own(c):
        return pltpu.make_async_copy(x.at[:, cols(c)], block(c, rows(me, 0, T)), own_sem.at[c])

    for c in range(last + 1):
        own(c).start()
    for i in range(3):
        tb_arrive(i)
        tb_copy(i + 4).start()
    arrive(0, AX, AY)
    start(0, FX, FY, PAX, PAY)
    start(1, AX, AY, BX, BY, PO)
    for i in range(3, 7):
        tb_arrive(i)
    for i in range(7):
        tb_copy(i).wait_send()

    eye = jnp.where(
        lax.broadcasted_iota(jnp.int32, (T, T), 0) == lax.broadcasted_iota(jnp.int32, (T, T), 1),
        1.0, 0.0).astype(BF16)
    row40 = lax.broadcasted_iota(jnp.int32, (SL, T), 0).astype(F32)
    row48 = lax.broadcasted_iota(jnp.int32, (PAD, T), 0).astype(F32)

    @pl.loop(0, 8)
    def _(s):
        mine = (lax.broadcasted_iota(jnp.int32, (8, T), 0) + me * 8).astype(F32)
        place = jnp.full((8, T), -1000.0, F32)
        share = jnp.zeros((8, T), F32)
        for j in range(8):
            hit = tables[s, j:j + 1, :] == mine
            place = jnp.where(hit, tables[s, 8 + j:9 + j, :], place)
            share = jnp.where(hit, tables[s, 16 + j:17 + j, :], share)
        for e in range(0, 8, 2):
            pick[s, e * SL:e * SL + PAIR, :] = jnp.concatenate(
                [jnp.where(row40 == place[i:i + 1, :], 1.0, 0.0) for i in (e, e + 1)], 0).astype(BF16)
        for e in range(8):
            zo[e * PAD:e * PAD + PAD, 0:T] = jnp.where(
                row48 == place[e:e + 1, :], share[e:e + 1, :], 0.0).astype(BF16)
        zo[pl.ds(pl.multiple_of(CH + s * T, T), T), 0:KP] = lax.dot_general(
            eye, zo[0:KP, 0:T], (((1,), (1,)), ((), ())), preferred_element_type=F32).astype(BF16)

    def mix_out(s):
        return pltpu.make_async_copy(
            zo.at[pl.ds(CH + s * T, T), pl.ds(0, KP)], y.at[:, pl.ds(s * KP, KP)], mix_sem.at[s])

    def mix_in(s):
        return pltpu.make_async_copy(
            y.at[:, pl.ds(s * KP, KP)],
            w2.at[1, pl.ds((s // 4) * T, T), pl.ds((s % 4) * KP, KP)], mix_sem.at[s])

    for s in range(8):
        mix_out(s).start()
    arrive(0, BX, BY)
    start(0, PBX, PBY)
    arrive(0, FX, FY)
    start(0, PFX, PFY)

    def gather(c):
        own(c).wait()
        arrive(c, PO, PAX, PAY, PBX, PBY, PFX, PFY)
        w_wait(c, 0)
        for p in range(4):
            a = dot(pick[2 * p], block(c, pl.ds(p * CH, T))[...])
            b = dot(pick[2 * p + 1], block(c, pl.ds(p * CH + T, T))[...])
            for e in range(8):
                zo[e * M + p * PAIR:e * M + p * PAIR + PAIR, 0:wide(c)] = jnp.concatenate(
                    [a[e * SL:e * SL + SL], b[e * SL:e * SL + SL]], 0).astype(BF16)

    for s in range(8):
        mix_out(s).wait()

    def pass_a(n):
        arrive(n, AX, AY)
        start(n, FX, FY, PAX, PAY)

    def pass_b(n):
        arrive(n, BX, BY)
        start(n, PBX, PBY)

    def pass_f(n):
        arrive(n, FX, FY)
        start(n, PFX, PFY)

    def of_expert(e):
        return pl.ds(e * M, M)

    def first(c):
        if not static(c):
            when(c > 1, lambda: sized(c + 1, pass_a, low=False))
        gather(c)
        k = pl.ds(0, wide(c))
        for pair in range(4):
            if pair:
                w_wait(c, pair)
            for e in (2 * pair, 2 * pair + 1):
                s = 2 * (e % 4)
                r = of_expert(e)
                z = zo[r, k]
                for n in range(0, acc_g.shape[1], CH):
                    nn = pl.ds(n, CH)
                    g = dot(z, slot_of(s)[k, nn])
                    u = dot(z, slot_of(s + 1)[k, nn])
                    if static(c):
                        acc_g[r, nn] = g
                        acc_u[r, nn] = u
                    else:
                        acc_g[r, nn] += g
                        acc_u[r, nn] += u
                w_next(c, e)
            if pair == 0 and static(c):
                pass_a(c + 1)
                start(c + 2, AX, AY)
            if pair == 0 and not static(c):
                @pl.when(c == 1)
                def _():
                    pass_a(2)
                    start(3, AX, AY)
            if pair == 1:
                sized(c + 2, lambda n: start(n, BX, BY, PO), low=False)
                if not static(c):
                    sized(c + 3, lambda n: start(n, AX, AY), low=False)
            if pair == (3 if static(c) else 2):
                sized(c + 1, pass_b, low=False)
                sized(c + 1, pass_f, low=False)

    first(0)
    pl.loop(1, last)(first)
    gather(last)

    def sent(c):
        for kind in range(13):
            ag_send(kind, c).wait_send()

    sent(0)
    pl.loop(1, last)(sent)
    sent(last)

    for mask in (4, 2, 1):
        pl.semaphore_signal(ready, inc=1, device_id=to(mask), device_id_type=MESH)

    def hidden(e, k):
        return xs.at[(e // 4) * 3 + k, pl.ds((e % 4) * M, M), :]

    for pair in range(4):
        if pair:
            w_wait(last, pair)
        for e in (2 * pair, 2 * pair + 1):
            s = 2 * (e % 4)
            r = of_expert(e)
            k = pl.ds(0, T)
            z = zo[r, k]
            for i in range(3):
                nn = pl.ds(i * CH, CH)
                g = acc_g[r, nn] + dot(z, slot_of(s)[k, nn])
                u = acc_u[r, nn] + dot(z, slot_of(s + 1)[k, nn])
                hidden(e, i)[...] = (jax.nn.silu(g) * u).astype(BF16)
        if pair < 2:
            w_fetch(last, pair + 2)
        else:
            for e in range(4 * pair - 8, min(4 * pair - 4, 6)):
                w_second(0, e)
    for s in range(8):
        mix_in(s).start()

    pl.semaphore_wait(ready, 3)

    chip = 2 * mx + my
    chip_x, chip_y, chip_d = 2 * (1 - mx) + my, 2 * mx + 1 - my, 3 - chip

    def part(d, i, first, n):
        k = d % 4
        r, c = (k % 2) * 2 * CH + i * T + first, (k // 2) * CH
        if not static(d):
            c = pl.multiple_of(c, CH)
        return acc_g.at[pl.ds(pl.multiple_of(r, H), n), pl.ds(c, wide(d))]

    def bank(slot, d, i):
        r = (d % 2) * 2 * CH + i * T
        if not (static(d) and static(i)):
            r = pl.multiple_of(r, T)
        return xs.at[slot, pl.ds(r, T), 0:wide(d)]

    def got_a(d, i):
        return bank(6, d, i)

    def put_a(d, i):
        return bank(7, d, i)

    def got(d, first, n):
        return xs.at[d % 4, pl.ds(LOW + first, n), 0:wide(d)]

    def put(d, first, n):
        return xs.at[4 + d % 2, pl.ds(LOW + first, n), 0:wide(d)]

    def send_a(d, i):
        return pltpu.make_async_remote_copy(
            src_ref=put_a(d, i), dst_ref=got_a(d, i), send_sem=a_s.at[d % 2, i], recv_sem=a_r.at[d % 2, i],
            device_id=to(1), device_id_type=MESH)

    def send_x1(d):
        return pltpu.make_async_remote_copy(
            src_ref=put(d, 0, T), dst_ref=got(d, 0, T), send_sem=sx_s.at[d % 2], recv_sem=t1_r.at[d % 4],
            device_id=to(4), device_id_type=MESH)

    def send_y1(d):
        return pltpu.make_async_remote_copy(
            src_ref=put(d, T, T), dst_ref=got(d, T, T), send_sem=sy_s.at[d % 2], recv_sem=t2_r.at[d % 4],
            device_id=to(2), device_id_type=MESH)

    def send_y2(d):
        return pltpu.make_async_remote_copy(
            src_ref=put(d, CH, H), dst_ref=got(d, CH, H), send_sem=cy_s.at[d % 2], recv_sem=ry_r.at[d % 4],
            device_id=to(2), device_id_type=MESH)

    def send_x2(d):
        return pltpu.make_async_remote_copy(
            src_ref=put(d, PT, H), dst_ref=got(d, PT, H), send_sem=cx_s.at[d % 2], recv_sem=rx_r.at[d % 4],
            device_id=to(4), device_id_type=MESH)

    def send_out(d):
        return [pltpu.make_async_copy(
            pick.at[2 * (d % 4) + n, pl.ds(0, T), :],
            y.at[:, pl.ds(cols(d).start + n * T, T)], ysem.at[d % 4, n])
            for n in range(wide(d) // T)]

    def step_b(d):
        for i in range(4):
            send_a(d, i).wait_recv()

        def free(n):
            send_x1(n).wait_send()
            send_y1(n).wait_send()

        def credit():
            pl.semaphore_wait(cred_x, 1)
            pl.semaphore_wait(cred_y, 1)

        if static(d):
            sized(d - 2, free)
        else:
            when(d == 2, lambda: free(0))
            when(d > 2, lambda: free(d - 2))
        when(d >= 4, credit)

        def total(i, first):
            return part(d, i, first, H)[...] + got_a(d, i)[pl.ds(first, H), :].astype(F32)

        put(d, 0, H)[...] = total(chip_x, 0).astype(BF16)
        put(d, H, H)[...] = total(chip_d, 0).astype(BF16)
        send_x1(d).start()
        put(d, T, H)[...] = total(chip_y, H).astype(BF16)
        put(d, KP, H)[...] = total(chip_d, H).astype(BF16)
        send_y1(d).start()
        for i, first in ((chip, 0), (chip, H), (chip_y, 0), (chip_x, H)):
            part(d, i, first, H)[...] = total(i, first)

        when(d < last - 1, lambda: pl.semaphore_signal(
            cred_p, inc=1, device_id=to(1), device_id_type=MESH))

    def step_c(d):
        def free(n):
            send_x2(n).wait_send()
            send_y2(n).wait_send()

        if static(d):
            sized(d - 2, free)
        else:
            when(d == 2, lambda: free(0))
            when(d > 2, lambda: free(d - 2))

        send_x1(d).wait_recv()
        put(d, CH, H)[...] = (part(d, chip_y, 0, H)[...] + got(d, H, H)[...].astype(F32)).astype(BF16)
        send_y2(d).start()
        send_y1(d).wait_recv()
        put(d, PT, H)[...] = (part(d, chip_x, H, H)[...] + got(d, KP, H)[...].astype(F32)).astype(BF16)
        send_x2(d).start()

    def step_d(d):
        def free(n):
            for copy in send_out(n):
                copy.wait()

        if static(d):
            sized(d - 4, free)
        else:
            when(d == 4, lambda: free(0))
            when(d > 4, lambda: free(d - 4))

        send_y2(d).wait_recv()
        top = part(d, chip, 0, H)[...] + got(d, 0, H)[...].astype(F32) + got(d, CH, H)[...].astype(F32)
        send_x2(d).wait_recv()
        low = part(d, chip, H, H)[...] + got(d, T, H)[...].astype(F32) + got(d, PT, H)[...].astype(F32)
        for n, copy in enumerate(send_out(d)):
            pick[2 * (d % 4) + n, 0:H, :] = top[:, n * T:n * T + T].astype(BF16)
            pick[2 * (d % 4) + n, H:T, :] = low[:, n * T:n * T + T].astype(BF16)
            copy.start()

        def give():
            pl.semaphore_signal(cred_x, inc=1, device_id=to(4), device_id_type=MESH)
            pl.semaphore_signal(cred_y, inc=1, device_id=to(2), device_id_type=MESH)

        when(d <= last - 4, give)

    def second(d):
        k = wide(d)
        for e in range(0, 8, 2):
            slots = [w_second_wait(d, e), w_second_wait(d, e + 1)]
            for i, s in zip((e, e + 1), slots):
                out = dot(hidden(i, 0)[...], w[s, :, pl.ds(0, k)])
                out += dot(hidden(i, 1)[...], w[s, :, pl.ds(CH, k)])
                out += dot(hidden(i, 2)[...], w[s, :, pl.ds(2 * CH, k)])
                for p in range(8):
                    piece = out[p * SL:p * SL + PAD] if p < 7 else jnp.concatenate(
                        [out[p * SL:], jnp.zeros((8, k), F32)], 0)
                    if p < 6:
                        zo[p * KP + i * PAD:p * KP + i * PAD + PAD, 0:k] = piece.astype(BF16)
                    else:
                        w2[0, i * PAD:i * PAD + PAD, pl.ds((p - 6) * CH, k)] = piece.astype(BF16)

            def more(n):
                for i in (e, e + 1):
                    w_second(n, (i + 6) % 8)
            if e == 0:
                more(d)
                sized(d - 1, step_b)
            else:
                sized(d + 1, more, low=False)

        def free(n):
            for i in range(4):
                send_a(n, i).wait_send()

        when(d >= 2, lambda: pl.semaphore_wait(cred_p, 1))
        if static(d):
            sized(d - 2, free)
        else:
            when(d == 2, lambda: free(0))
            when(d > 2, lambda: free(d - 2))

        if static(d) and d == 0:
            for s in range(8):
                mix_in(s).wait()

        def mixed(i, c):
            s = 2 * i + c
            mix = w2[1, pl.ds((i // 2) * T, T), pl.ds(pl.multiple_of((2 * (i % 2) + c) * KP, H), KP)]
            if i == 3:
                return dot(mix, w2[0, 0:KP, pl.ds(pl.multiple_of(c * CH, CH), k)])
            return dot(mix, zo[pl.ds(pl.multiple_of(s * KP, KP), KP), 0:k])

        for i in range(4):
            put_a(d, i)[...] = mixed(i, 1 - mc).astype(BF16)
            send_a(d, i).start()
        for i in range(4):
            part(d, i, 0, T)[...] = mixed(i, mc)

        if static(d):
            sized(d - 2, step_c)
            sized(d - 3, step_d)
        else:
            when(d == 2, lambda: step_c(0))
            when(d > 2, lambda: step_c(d - 2))
            when(d == 3, lambda: step_d(0))
            when(d > 3, lambda: step_d(d - 3))

    second(0)
    pl.loop(1, last)(second)
    second(last)
    step_b(last)
    step_c(last - 1)
    step_d(last - 2)
    step_c(last)
    step_d(last - 1)
    step_d(last)
    for d in (last - 1, last):
        for i in range(4):
            send_a(d, i).wait_send()
        for copy in (send_x1(d), send_y1(d), send_x2(d), send_y2(d)):
            copy.wait_send()
    for d in range(last - 3, last + 1):
        for copy in send_out(d):
            copy.wait()


def solution(mesh):
    def body(x, expert, slot, gate, w_gate, w_up, w_down):
        tokens, dim = x.shape[2:]
        ff = w_gate.shape[2]
        dma = pltpu.SemaphoreType.DMA
        any_ = pl.BlockSpec(memory_space=pl.ANY)
        y = pl.pallas_call(
            kernel,
            out_shape=jax.ShapeDtypeStruct((tokens, dim), BF16),
            in_specs=[any_] + [pl.BlockSpec(memory_space=pltpu.VMEM)] * 3 + [any_] * 3,
            out_specs=any_,
            scratch_shapes=[
                pltpu.VMEM((dim // CH, 8 * tokens, CH), BF16),
                pltpu.VMEM((ROWS, ff), F32),
                pltpu.VMEM((ROWS, ff), F32),
                pltpu.VMEM((ROWS, CH), BF16),
                pltpu.VMEM((8, M, T), BF16),
                pltpu.VMEM((NW, CH, ff), BF16),
                pltpu.VMEM((2, CH, ff), BF16),
                pltpu.VMEM((8, TAB, T), F32),
                dma((13, dim // CH + 1)), dma((13, dim // CH + 1)), dma((7,)), dma((7,)),
                dma((dim // CH + 1,)), dma((8,)), dma((NW + 2,)),
                dma((2, 4)), dma((2, 4)), dma((2,)), dma((2,)), dma((4,)), dma((4,)),
                dma((2,)), dma((2,)), dma((4,)), dma((4,)), dma((4, 2)),
                pltpu.SemaphoreType.REGULAR, pltpu.SemaphoreType.REGULAR,
                pltpu.SemaphoreType.REGULAR, pltpu.SemaphoreType.REGULAR,
            ],
            compiler_params=pltpu.CompilerParams(
                collective_id=0, has_side_effects=True, vmem_limit_bytes=67043328),
        )(x[0, 0], expert[0, 0].T, slot[0, 0].T, gate[0, 0].T, w_gate, w_up, w_down)
        return y[None, None]

    tok = P("dp", "ep", None, None)
    wt = P("ep", None, None)
    return jax.shard_map(
        body, mesh=mesh, in_specs=(tok, tok, tok, tok, wt, wt, wt), out_specs=tok, check_vma=False
    )
```

time: 194 us -> 185 us (0.954)
  Pallas kernels: 187 us -> 182 us
  other arithmetic: 2.71 us -> 0 us
    pallas_call x1, Pallas kernels: 187 us -> 182 us  [body(): pl.pallas_call(kernel, out_shape=jax.ShapeDtypeStruct((tokens, dim), BF16...]
    transpose x3 -> x0, other arithmetic: 2.1 us -> none  [the longest x1 0.7 us: body(): jnp.where(keep, slot[0, 0], -1000).astype(F32)]
where the time goes in v1:
time: 185 us
  Pallas kernels  182 us (98%)
  local copies, waits for them, and re-layouts  3.13 us (2%)
    pallas_call x1, Pallas kernels, body(): pl.pallas_call(kernel, out_shape=jax.ShapeDtypeStruct((tokens, dim), BF16...  182 us

profile of v1, /device:TPU:0, one launch (start us, length us, event | category | flops | bytes accessed | tf_op | source)
XLA Modules:
  0.0 185.3 jit_solution(10356939107081247884)
XLA Ops:
  0.0 182.1 %shard_map.73 = bf16[256,4096]{1,0:T(8,128)(2,1)} custom-call(bf16[256,4096]{1,0:T(8,128)(2,1)} %bitcast.12, s32[8,256]{1,0:T(8,128)} %bitcast.13, s32[8,256]{1,0:T(8,128)} %bitcast.14, f32[8,256]{1,0:T(8,128)} %bitcast.15, bf16[8,4096,1536]{2,1,0:T(8,128)(2,1)} %wg.1, bf16[8,4096,1536]{2,1,0:T(8,128)(2,1)} %wu.1, bf16[8,1536,4096]{2,1,0:T(8,128)(2,1)} %wd.1), custom_call_target="tpu_custom_call" | custom-call | tf_op jit(solution)/shard_map/pallas_call | solution.py:565
  182.1 3.1 %copy.9 = bf16[1,1,256,4096]{3,2,1,0:T(8,128)(2,1)} copy(bf16[1,1,256,4096]{3,2,1,0:T(8,128)(2,1)} %bitcast.11) | data formatting | bytes 4194304
